TPU v7x, 32 devices: a whole 2x2x4 slice. The times are simulated.
32 devices in a mesh: group: 2 (over y), ha: 4 (over x, core), wa: 4 (over z).
Axes of the slice: x: 2, y: 2, z: 4, core: 2. Of those that a mesh axis runs over, the one named last changes fastest.
Arguments:
- queries: bfloat16 [4, 32, 32, 1536], P('group', 'ha', 'wa'), parts along dimension 0, may hold values from -6 to 6
- keys: bfloat16 [4, 32, 32, 1536], P('group', 'ha', 'wa'), parts along dimension 0, may hold values from -6 to 6
- values: bfloat16 [4, 32, 32, 1536], P('group', 'ha', 'wa'), parts along dimension 0, may hold values from -6 to 6
- out_grad: bfloat16 [4, 32, 32, 1536], P('group', 'ha', 'wa'), parts along dimension 0, may hold values from -96 to 96
- log_norm: float32 [12, 4, 32, 32], P(None, 'group', 'ha', 'wa'), parts along dimension 1, may hold values from 6.5 to 7.5
- delta_rows: float32 [12, 4, 32, 32], P(None, 'group', 'ha', 'wa'), parts along dimension 1, may hold values from -360 to 360
- text_keys: bfloat16 [64, 1536], P('group'), parts along dimension 0, may hold values from -6 to 6
- text_values: bfloat16 [64, 1536], P('group'), parts along dimension 0, may hold values from -6 to 6
- window_table: int32 [4, 4, 9], replicated, may hold values 0 or 1
Outputs:
- query_grad: bfloat16 [4, 32, 32, 1536], P('group', 'ha', 'wa'), parts along dimension 0
- key_grad: bfloat16 [4, 32, 32, 1536], P('group', 'ha', 'wa'), parts along dimension 0
- value_grad: bfloat16 [4, 32, 32, 1536], P('group', 'ha', 'wa'), parts along dimension 0
- text_key_grad: bfloat16 [64, 1536], P('group'), parts along dimension 0
- text_value_grad: bfloat16 [64, 1536], P('group'), parts along dimension 0
There are 2 independent parts, one for each index of `group`. A program takes and returns all parts, laid end to end along the dimension named above; an argument that names none is the same for every part. Nothing has to cross between parts.
All inputs are finite; a program needn't handle non-finite values.
Results may differ from a plain program's by a relative error of at most 0.001.
The roundings to bfloat16 on the way count: a program that leaves them out, or rounds other values in their place, can miss the bound.
Values may be sent and summed in bfloat16 or wider, within the bound.
A program may use at most 64 MiB of HBM per device.

v0:
```python
import math

import jax
import jax.numpy as jnp
from jax import lax
from jax.sharding import PartitionSpec as P

HEADS = 12
HDIM = 128
TILE = 8
HALO = 2


def passed_along(value, axis, steps):
    count = lax.axis_size(axis)
    pairs = [(source, (source + steps) % count) for source in range(count)]
    return lax.ppermute(value, axis, pairs)


def with_halo(cells, sides, width):
    for axis, dim in sides:
        count = lax.axis_size(axis)
        head = lax.slice_in_dim(cells, 0, width, axis=dim)
        tail = lax.slice_in_dim(cells, cells.shape[dim] - width, cells.shape[dim], axis=dim)
        cells = jnp.concatenate(
            [
                lax.ppermute(tail, axis, [(i, (i + 1) % count) for i in range(count)]),
                cells,
                lax.ppermute(head, axis, [((i + 1) % count, i) for i in range(count)]),
            ],
            axis=dim,
        )
    return cells


def tile_grads(query_rows, cotangent_rows, norm_rows, delta_part, key_rows, value_rows, cell_mask):
    score_scale = 1.0 / math.sqrt(query_rows.shape[-1])
    scores = (
        jnp.einsum("qhd,khd->hqk", query_rows, key_rows, preferred_element_type=jnp.float32)
        * score_scale
    )
    probs = jnp.exp(scores - norm_rows[:, :, None])
    if cell_mask is not None:
        probs = probs * cell_mask[None, None, :]
    probs_half = probs.astype(jnp.bfloat16)
    value_part = jnp.einsum(
        "hqk,qhd->khd", probs_half, cotangent_rows, preferred_element_type=jnp.float32
    )
    prob_grad = jnp.einsum(
        "qhd,khd->hqk", cotangent_rows, value_rows, preferred_element_type=jnp.float32
    )
    score_grad = (probs * (prob_grad - delta_part[:, :, None])).astype(jnp.bfloat16)
    query_part = (
        jnp.einsum("hqk,khd->qhd", score_grad, key_rows, preferred_element_type=jnp.float32)
        * score_scale
    )
    key_part = (
        jnp.einsum("hqk,qhd->khd", score_grad, query_rows, preferred_element_type=jnp.float32)
        * score_scale
    )
    return (query_part, key_part, value_part)


def send_cols(strip, offset):
    return passed_along(strip, "wa", offset)


def send_rows(strip, offset):
    return passed_along(strip, "ha", offset)


def fold_band(buffer, along, mover):
    lower = lax.slice_in_dim(buffer, 0, HALO, axis=along)
    middle = lax.slice_in_dim(buffer, HALO, HALO + TILE, axis=along)
    upper = lax.slice_in_dim(buffer, HALO + TILE, TILE + 2 * HALO, axis=along)
    from_before = mover(upper, 1)
    from_after = mover(lower, -1)
    widths_low = [(0, 0)] * buffer.ndim
    widths_high = [(0, 0)] * buffer.ndim
    widths_low[along] = (0, TILE - HALO)
    widths_high[along] = (TILE - HALO, 0)
    return middle + jnp.pad(from_before, widths_low) + jnp.pad(from_after, widths_high)


def local(
    queries, keys, values, out_grad, log_norm, delta_rows, text_keys, text_values, window_table
):
    frames, tile_side, _, width = queries.shape
    window_side = TILE + 2 * HALO
    stacked = jnp.stack((keys, values))
    window = with_halo(stacked, (("ha", 2), ("wa", 3)), HALO)
    row_tile = lax.axis_index("ha")
    col_tile = lax.axis_index("wa")
    anchor = jnp.zeros((), jnp.int32)
    pattern = (
        lax.dynamic_slice(window_table, (row_tile, col_tile, anchor), (1, 1, 9))
        .reshape(3, 3)
        .astype(jnp.float32)
    )
    position = jnp.arange(window_side, dtype=jnp.int32)
    block_of = (position >= HALO).astype(jnp.int32) + (position >= HALO + TILE).astype(jnp.int32)
    one_hot = (block_of[:, None] == jnp.arange(3, dtype=jnp.int32)[None, :]).astype(jnp.float32)
    cell_grid = jnp.dot(
        jnp.dot(one_hot, pattern, precision=lax.Precision.HIGHEST),
        one_hot.T,
        precision=lax.Precision.HIGHEST,
    )
    cell_mask = jnp.broadcast_to(cell_grid[None], (frames, window_side, window_side)).reshape(-1)
    query_rows = queries.reshape(-1, HEADS, HDIM)
    cotangent_rows = out_grad.reshape(-1, HEADS, HDIM)
    norm_rows = log_norm.reshape(HEADS, -1)
    delta_part = delta_rows.reshape(HEADS, -1)
    key_rows = window[0].reshape(-1, HEADS, HDIM)
    value_rows = window[1].reshape(-1, HEADS, HDIM)
    video_query, video_key, video_value = tile_grads(
        query_rows, cotangent_rows, norm_rows, delta_part, key_rows, value_rows, cell_mask
    )
    text_query, text_key, text_value = tile_grads(
        query_rows,
        cotangent_rows,
        norm_rows,
        delta_part,
        text_keys.reshape(-1, HEADS, HDIM),
        text_values.reshape(-1, HEADS, HDIM),
        None,
    )
    query_grad = (
        (video_query + text_query).astype(jnp.bfloat16).reshape(frames, tile_side, tile_side, width)
    )
    text_total = lax.psum(jnp.stack((text_key, text_value)), ("ha", "wa"))
    buffer = jnp.stack((video_key, video_value)).reshape(2, frames, window_side, window_side, width)
    buffer = fold_band(buffer, 2, send_rows)
    buffer = fold_band(buffer, 3, send_cols)
    text_key_grad = text_total[0].reshape(-1, width).astype(jnp.bfloat16)
    text_value_grad = text_total[1].reshape(-1, width).astype(jnp.bfloat16)
    return (
        query_grad,
        buffer[0].astype(jnp.bfloat16),
        buffer[1].astype(jnp.bfloat16),
        text_key_grad,
        text_value_grad,
    )


def solution(mesh):
    in_specs = (
        P("group", "ha", "wa", None),
        P("group", "ha", "wa", None),
        P("group", "ha", "wa", None),
        P("group", "ha", "wa", None),
        P(None, "group", "ha", "wa"),
        P(None, "group", "ha", "wa"),
        P("group", None),
        P("group", None),
        P(),
    )
    out_specs = (
        P("group", "ha", "wa", None),
        P("group", "ha", "wa", None),
        P("group", "ha", "wa", None),
        P("group", None),
        P("group", None),
    )
    return jax.shard_map(local, mesh=mesh, in_specs=in_specs, out_specs=out_specs, check_vma=False)
```

profile of v0, /device:TPU:0, one launch (start us, length us, event | category | flops | bytes accessed | tf_op | source)
XLA Modules:
  0.0 151.5 jit_solution(18392472798687320180)
XLA Ops:
  0.7 1.1 pad_maximum_fusion.7
  2.4 2.0 %collective-permute-start.1 = (bf16[2,2,2,8,1536]{4,3,2,1,0:T(8,128)(2,1)S(1)}, bf16[2,2,2,8,1536]{4,3,2,1,0:T(8,128)(2,1)S(1)}, u32[]{:S(2)}, u32[]{:S(2)}) collective-permute-start(bf16[2,2,2,8,1536]{4,3,2,1,0:T(8,128)(2,1)S(1)} %get-tuple-element.21), channel_id=1, source_target_pairs={{4,0},{8,4},{12,8},{0,12},{5,1},{9,5},{13,9},{1,13},{6,2},{10,6},{... | collective-permute-start | bytes 589832 | tf_op jit(solution)/shard_map/ppermute | solution.py:29
  7.4 1.4 reshape.49
  11.0 1.2 pad_maximum_fusion.5
  12.1 2.3 %collective-permute-start.2 = (bf16[2,2,12,2,1536]{4,3,2,1,0:T(2,128)(2,1)}, bf16[2,2,12,2,1536]{4,3,2,1,0:T(2,128)(2,1)S(1)}, u32[]{:S(2)}, u32[]{:S(2)}) collective-permute-start(bf16[2,2,12,2,1536]{4,3,2,1,0:T(2,128)(2,1)} %get-tuple-element.16), channel_id=1, source_target_pairs={{0,1},{1,2},{2,3},{3,0},{4,5},{5,6},{6,7},{7,4},{8,9},{9,10},{10,1... | collective-permute-start | bytes 884744 | tf_op jit(solution)/shard_map/ppermute | solution.py:27
  14.5 2.0 %collective-permute-start.3 = (bf16[2,2,12,2,1536]{4,3,2,1,0:T(2,128)(2,1)}, bf16[2,2,12,2,1536]{4,3,2,1,0:T(2,128)(2,1)S(1)}, u32[]{:S(2)}, u32[]{:S(2)}) collective-permute-start(bf16[2,2,12,2,1536]{4,3,2,1,0:T(2,128)(2,1)} %get-tuple-element.17), channel_id=1, source_target_pairs={{1,0},{2,1},{3,2},{0,3},{5,4},{6,5},{7,6},{4,7},{9,8},{10,9},{11,1... | collective-permute-start | bytes 884744 | tf_op jit(solution)/shard_map/ppermute | solution.py:29
  16.5 73.5 %all-reduce.5 = bf16[2,32,12,128]{3,1,2,0:T(8,128)(2,1)} all-reduce(f32[2,32,12,128]{3,1,2,0:T(8,128)S(1)} %pad_maximum_fusion.1), channel_id=1, replica_groups=mesh['group'=2,'ha'=4,'wa'=4] {'ha','wa'}, use_global_device_ids=true, to_apply=%region_0.0 | all-reduce | flops 98304 | bytes 589824 | tf_op jit(solution)/shard_map/psum | solution.py:130
  90.0 1.5 pad_maximum_fusion
  91.7 1.7 %reshape_squeeze.9 = bf16[288,12,128]{2,1,0:T(8,128)(2,1)} reshape(bf16[1,2,12,12,1536]{4,3,2,1,0:T(8,128)(2,1)S(1)} %get-tuple-element.14) | data formatting | bytes 1769472 | tf_op jit(solution)/shard_map/reshape;squeeze | solution.py:114
  94.7 1.6 %convolution_bitcast_fusion = f32[288,12,128]{2,0,1:T(8,128)} fusion(f32[12,288,128]{2,1,0:T(8,128)S(1)} %exponential_multiply_fusion, bf16[128,12,128]{2,1,0:T(8,128)(2,1)S(1)} %reshape.50), kind=kOutput, calls=%fused_computation.9 | convolution fusion | flops 113688576 | bytes 3932160 | tf_op jit(solution)/shard_map/hqk,qhd->khd/dot_general | solution.py:46
  97.8 2.5 %copy.75 = f32[288,12,128]{2,1,0:T(8,128)} copy(f32[288,12,128]{2,0,1:T(8,128)S(1)} %multiply_bitcast_fusion) | data formatting | bytes 3538944 | tf_op jit(solution)/shard_map/mul | solution.py:58
  100.3 2.4 %stack.30 = f32[1,2,12,12,1536]{4,3,2,1,0:T(8,128)S(1)} reshape(f32[288,12,128]{2,1,0:T(8,128)} %copy.75) | data formatting | bytes 3538944 | tf_op jit(solution)/shard_map/stack | solution.py:131
  102.7 4.0 %copy.77 = f32[288,12,128]{2,1,0:T(8,128)} copy(f32[288,12,128]{2,0,1:T(8,128)} %convolution_bitcast_fusion) | data formatting | bytes 3538944 | tf_op jit(solution)/shard_map/hqk,qhd->khd/transpose | solution.py:46
  106.6 3.2 %stack.31 = f32[1,2,12,12,1536]{4,3,2,1,0:T(8,128)} reshape(f32[288,12,128]{2,1,0:T(8,128)} %copy.77) | data formatting | bytes 3538944 | tf_op jit(solution)/shard_map/stack | solution.py:131
  110.1 1.4 copy-done.1
  114.2 12.1 %collective-permute-done.5 = f32[2,2,2,12,1536]{4,2,3,1,0:T(2,128)S(1)} collective-permute-done((f32[2,2,2,12,1536]{4,2,3,1,0:T(2,128)S(1)}, f32[2,2,2,12,1536]{4,2,3,1,0:T(2,128)S(1)}, u32[]{:S(2)}, u32[]{:S(2)}) %collective-permute-start.5) | collective-permute-done | bytes 589856 | tf_op jit(solution)/shard_map/ppermute | solution.py:17
  126.4 1.4 collective-permute-done.4
  128.4 1.2 fusion.37
  129.6 3.8 %collective-permute-start.7 = (f32[2,2,8,2,1536]{4,3,2,1,0:T(2,128)}, f32[2,2,8,2,1536]{4,3,2,1,0:T(2,128)}, u32[]{:S(2)}, u32[]{:S(2)}) collective-permute-start(f32[2,2,8,2,1536]{4,3,2,1,0:T(2,128)} %get-tuple-element.13), channel_id=1, source_target_pairs={{0,3},{1,0},{2,1},{3,2},{4,7},{5,4},{6,5},{7,6},{8,11},{9,8},{10,9... | collective-permute-start | bytes 1179656 | tf_op jit(solution)/shard_map/ppermute | solution.py:17
  135.1 2.2 %copy.73 = bf16[128,12,128]{2,1,0:T(8,128)(2,1)} copy(bf16[128,12,128]{0,2,1:T(8,128)(2,1)} %fusion.6) | data formatting | bytes 786432 | tf_op jit(solution)/shard_map/convert_element_type | solution.py:128
  137.3 2.1 %reshape.53 = bf16[2,8,8,1536]{3,2,1,0:T(8,128)(2,1)} reshape(bf16[128,12,128]{2,1,0:T(8,128)(2,1)} %copy.73) | data formatting | bytes 786432 | tf_op jit(solution)/shard_map/reshape | solution.py:128
  139.4 4.4 %collective-permute-done.6 = f32[2,2,8,2,1536]{4,3,2,1,0:T(2,128)} collective-permute-done((f32[2,2,8,2,1536]{4,3,2,1,0:T(2,128)}, f32[2,2,8,2,1536]{4,3,2,1,0:T(2,128)}, u32[]{:S(2)}, u32[]{:S(2)}) %collective-permute-start.6) | collective-permute-done | bytes 393248 | tf_op jit(solution)/shard_map/ppermute | solution.py:17
  143.7 5.2 %collective-permute-done.7 = f32[2,2,8,2,1536]{4,3,2,1,0:T(2,128)} collective-permute-done((f32[2,2,8,2,1536]{4,3,2,1,0:T(2,128)}, f32[2,2,8,2,1536]{4,3,2,1,0:T(2,128)}, u32[]{:S(2)}, u32[]{:S(2)}) %collective-permute-start.7) | collective-permute-done | bytes 393248 | tf_op jit(solution)/shard_map/ppermute | solution.py:17
  149.0 1.6 %fusion.2 = bf16[2,2,8,8,1536]{4,3,2,1,0:T(8,128)(2,1)S(1)} fusion(f32[2,2,8,12,1536]{4,3,2,1,0:T(8,128)S(1)} %fusion, f32[2,2,8,2,1536]{4,3,2,1,0:T(2,128)} %collective-permute-done.7, f32[2,2,8,2,1536]{4,3,2,1,0:T(2,128)} %collective-permute-done.6), kind=kLoop, calls=%fused_computation.8 | loop fusion | flops 1179648 | bytes 3145728 | tf_op jit(solution)/shard_map/convert.3
  (70 shorter events, 14.8 us)
Async XLA Ops:
  0.6 8.4 %copy-start = (bf16[32,1536]{1,0:T(8,128)(2,1)S(1)}, bf16[32,1536]{1,0:T(8,128)(2,1)}, u32[]{:S(2)}) copy-start(bf16[32,1536]{1,0:T(8,128)(2,1)} %param.15) | copy-start | bytes 294916
  0.6 8.1 %copy-start.12 = (bf16[2,8,8,1536]{3,2,1,0:T(8,128)(2,1)S(1)}, bf16[2,8,8,1536]{3,2,1,0:T(8,128)(2,1)}, u32[]{:S(2)}) copy-start(bf16[2,8,8,1536]{3,2,1,0:T(8,128)(2,1)} %param.12) | copy-start | bytes 1179652
  0.7 8.7 %copy-start.13 = (bf16[32,1536]{1,0:T(8,128)(2,1)S(1)}, bf16[32,1536]{1,0:T(8,128)(2,1)}, u32[]{:S(2)}) copy-start(bf16[32,1536]{1,0:T(8,128)(2,1)} %param.16) | copy-start | bytes 294916
  1.8 9.1 %collective-permute-start = (bf16[2,2,2,8,1536]{4,3,2,1,0:T(8,128)(2,1)S(1)}, bf16[2,2,2,8,1536]{4,3,2,1,0:T(8,128)(2,1)S(1)}, u32[]{:S(2)}, u32[]{:S(2)}) collective-permute-start(bf16[2,2,2,8,1536]{4,3,2,1,0:T(8,128)(2,1)S(1)} %get-tuple-element.20), channel_id=1, source_target_pairs={{0,4},{4,8},{8,12},{12,0},{1,5},{5,9},{9,13},{13,1},{2,6},{6,10},{... | collective-permute-start | bytes 589832 | tf_op jit(solution)/shard_map/ppermute | solution.py:27
  2.4 8.6 %collective-permute-start.1 = (bf16[2,2,2,8,1536]{4,3,2,1,0:T(8,128)(2,1)S(1)}, bf16[2,2,2,8,1536]{4,3,2,1,0:T(8,128)(2,1)S(1)}, u32[]{:S(2)}, u32[]{:S(2)}) collective-permute-start(bf16[2,2,2,8,1536]{4,3,2,1,0:T(8,128)(2,1)S(1)} %get-tuple-element.21), channel_id=1, source_target_pairs={{4,0},{8,4},{12,8},{0,12},{5,1},{9,5},{13,9},{1,13},{6,2},{10,6},{... | collective-permute-start | bytes 589832 | tf_op jit(solution)/shard_map/ppermute | solution.py:29
  7.4 3.6 %copy-start.7 = (bf16[2,8,8,1536]{3,2,1,0:T(8,128)(2,1)S(1)}, bf16[2,8,8,1536]{3,2,1,0:T(8,128)(2,1)}, u32[]{:S(2)}) copy-start(bf16[2,8,8,1536]{3,2,1,0:T(8,128)(2,1)} %param.11) | copy-start | bytes 1179652
  7.4 3.6 %copy-start.8 = (bf16[2,8,8,1536]{3,2,1,0:T(8,128)(2,1)S(1)}, bf16[2,8,8,1536]{3,2,1,0:T(8,128)(2,1)}, u32[]{:S(2)}) copy-start(bf16[2,8,8,1536]{3,2,1,0:T(8,128)(2,1)} %param.10) | copy-start | bytes 1179652
  9.7 0.7 copy-start.9
  12.1 77.9 %collective-permute-start.2 = (bf16[2,2,12,2,1536]{4,3,2,1,0:T(2,128)(2,1)}, bf16[2,2,12,2,1536]{4,3,2,1,0:T(2,128)(2,1)S(1)}, u32[]{:S(2)}, u32[]{:S(2)}) collective-permute-start(bf16[2,2,12,2,1536]{4,3,2,1,0:T(2,128)(2,1)} %get-tuple-element.16), channel_id=1, source_target_pairs={{0,1},{1,2},{2,3},{3,0},{4,5},{5,6},{6,7},{7,4},{8,9},{9,10},{10,1... | collective-permute-start | bytes 884744 | tf_op jit(solution)/shard_map/ppermute | solution.py:27
  14.5 75.5 %collective-permute-start.3 = (bf16[2,2,12,2,1536]{4,3,2,1,0:T(2,128)(2,1)}, bf16[2,2,12,2,1536]{4,3,2,1,0:T(2,128)(2,1)S(1)}, u32[]{:S(2)}, u32[]{:S(2)}) collective-permute-start(bf16[2,2,12,2,1536]{4,3,2,1,0:T(2,128)(2,1)} %get-tuple-element.17), channel_id=1, source_target_pairs={{1,0},{2,1},{3,2},{0,3},{5,4},{6,5},{7,6},{4,7},{9,8},{10,9},{11,1... | collective-permute-start | bytes 884744 | tf_op jit(solution)/shard_map/ppermute | solution.py:29
  94.1 2.2 %copy-start.4 = (bf16[288,12,128]{2,1,0:T(8,128)(2,1)}, bf16[288,12,128]{2,1,0:T(8,128)(2,1)S(1)}, u32[]{:S(2)}) copy-start(bf16[288,12,128]{2,1,0:T(8,128)(2,1)S(1)} %reshape_squeeze.8) | copy-start | bytes 2654212
  94.7 1.6 %copy-start.6 = (bf16[288,12,128]{2,1,0:T(8,128)(2,1)S(1)}, bf16[288,12,128]{2,1,0:T(8,128)(2,1)}, u32[]{:S(2)}) copy-start(bf16[288,12,128]{2,1,0:T(8,128)(2,1)} %reshape_squeeze.9) | copy-start | bytes 2654212
  96.8 0.9 copy-start.2
  109.8 1.7 %copy-start.1 = (f32[1,2,12,12,1536]{4,3,2,1,0:T(8,128)S(1)}, f32[1,2,12,12,1536]{4,3,2,1,0:T(8,128)}, u32[]{:S(2)}) copy-start(f32[1,2,12,12,1536]{4,3,2,1,0:T(8,128)} %stack.31) | copy-start | bytes 5308420
  111.7 1.6 %copy-start.11 = (bf16[2,32,12,128]{3,1,2,0:T(8,128)(2,1)S(1)}, bf16[2,32,12,128]{3,1,2,0:T(8,128)(2,1)}, u32[]{:S(2)}) copy-start(bf16[2,32,12,128]{3,1,2,0:T(8,128)(2,1)} %all-reduce.5) | copy-start | bytes 589828
  112.8 13.5 %collective-permute-start.5 = (f32[2,2,2,12,1536]{4,2,3,1,0:T(2,128)S(1)}, f32[2,2,2,12,1536]{4,2,3,1,0:T(2,128)S(1)}, u32[]{:S(2)}, u32[]{:S(2)}) collective-permute-start(f32[2,2,2,12,1536]{4,2,3,1,0:T(2,128)S(1)} %copy.80), channel_id=1, source_target_pairs={{0,12},{4,0},{8,4},{12,8},{1,13},{5,1},{9,5},{13,9},{2,14},{6,2},{... | collective-permute-start | bytes 1769480 | tf_op jit(solution)/shard_map/ppermute | solution.py:17
  112.9 15.0 %collective-permute-start.4 = (f32[2,2,2,12,1536]{4,2,3,1,0:T(2,128)S(1)}, f32[2,2,2,12,1536]{4,2,3,1,0:T(2,128)S(1)}, u32[]{:S(2)}, u32[]{:S(2)}) collective-permute-start(f32[2,2,2,12,1536]{4,2,3,1,0:T(2,128)S(1)} %copy.78), channel_id=1, source_target_pairs={{0,4},{4,8},{8,12},{12,0},{1,5},{5,9},{9,13},{13,1},{2,6},{6,10},{... | collective-permute-start | bytes 1769480 | tf_op jit(solution)/shard_map/ppermute | solution.py:17
  128.0 5.5 %copy-start.3 = (bf16[12,288,128]{2,1,0:T(8,128)(2,1)S(1)}, bf16[12,288,128]{2,1,0:T(8,128)(2,1)}, u32[]{:S(2)}) copy-start(bf16[12,288,128]{2,1,0:T(8,128)(2,1)} %copy-done.2) | copy-start | bytes 2654212
  128.0 5.4 %copy-start.5 = (bf16[288,12,128]{2,1,0:T(8,128)(2,1)S(1)}, bf16[288,12,128]{2,1,0:T(8,128)(2,1)}, u32[]{:S(2)}) copy-start(bf16[288,12,128]{2,1,0:T(8,128)(2,1)} %copy-done.4) | copy-start | bytes 2654212
  128.4 5.6 %copy-start.10 = (bf16[12,128,32]{1,2,0:T(8,128)(2,1)S(1)}, bf16[12,128,32]{1,2,0:T(8,128)(2,1)}, u32[]{:S(2)}) copy-start(bf16[12,128,32]{1,2,0:T(8,128)(2,1)} %copy-done.9) | copy-start | bytes 294916
  129.6 14.1 %collective-permute-start.6 = (f32[2,2,8,2,1536]{4,3,2,1,0:T(2,128)}, f32[2,2,8,2,1536]{4,3,2,1,0:T(2,128)}, u32[]{:S(2)}, u32[]{:S(2)}) collective-permute-start(f32[2,2,8,2,1536]{4,3,2,1,0:T(2,128)} %get-tuple-element.12), channel_id=1, source_target_pairs={{0,1},{1,2},{2,3},{3,0},{4,5},{5,6},{6,7},{7,4},{8,9},{9,10},{10,1... | collective-permute-start | bytes 1179656 | tf_op jit(solution)/shard_map/ppermute | solution.py:17
  129.6 19.3 %collective-permute-start.7 = (f32[2,2,8,2,1536]{4,3,2,1,0:T(2,128)}, f32[2,2,8,2,1536]{4,3,2,1,0:T(2,128)}, u32[]{:S(2)}, u32[]{:S(2)}) collective-permute-start(f32[2,2,8,2,1536]{4,3,2,1,0:T(2,128)} %get-tuple-element.13), channel_id=1, source_target_pairs={{0,3},{1,0},{2,1},{3,2},{4,7},{5,4},{6,5},{7,6},{8,11},{9,8},{10,9... | collective-permute-start | bytes 1179656 | tf_op jit(solution)/shard_map/ppermute | solution.py:17
where the time goes:
time: 152 us; the launch traced here: 151 us
  blocking collectives  73.5 us (48%)
  local copies, waits for them, and re-layouts  30 us (20%)
  waiting for transfers between devices  23.1 us (15%)
  starting transfers between devices  11.3 us (7%)
  other arithmetic  6.52 us (4%)
  matrix products  6.17 us (4%)
    psum x1, blocking collectives, local(): text_total = lax.psum(jnp.stack((text_key, text_value)), ('ha', 'wa'))  73.5 us
    ppermute x4, waiting for transfers between devices, passed_along(): return lax.ppermute(value, axis, pairs)  23.1 us
    another operation x3, local copies, waits for them, and re-layouts, local(): jnp.stack((video_key, video_value))  5.81 us
    ppermute x4, starting transfers between devices, passed_along(): return lax.ppermute(value, axis, pairs)  4.38 us
    ppermute x2, starting transfers between devices, with_halo(): lax.ppermute(head, axis, [((i + 1) % count, i) for i in range(count)])  4.01 us
    transpose x1, local copies, waits for them, and re-layouts, tile_grads(): jnp.einsum('hqk,qhd->khd', probs_half, cotangent_rows, preferred_element_...  3.98 us
  transfers between devices with their start and end apart: 8, of which 4 were waited for; matrix products, arithmetic and copies ran while one was open for 8% of the time, Pallas kernels for 0%

commit v1 on v0

v1 whole, which is shorter than its diff:
```python
import functools
import math

import jax
import jax.numpy as jnp
from jax import lax
from jax.experimental import pallas as pl
from jax.experimental.pallas import tpu as pltpu
from jax.sharding import PartitionSpec as P

HDIM = 128
HALO = 2
GROUPS = 4
MESH = pl.DeviceIdType.MESH
F32 = jnp.float32
BF16 = jnp.bfloat16


def text_plan(n_ha, n_wa, blocks, width):
    plan = []
    for axis, count in (("ha", n_ha), ("wa", n_wa)):
        far = 1
        while far < count:
            if blocks > 1:
                blocks //= 2
                plan.append((axis, far, blocks, width, "rows"))
            elif width % 256 == 0:
                width //= 2
                plan.append((axis, far, blocks, width, "cols"))
            else:
                plan.append((axis, far, blocks, width, "none"))
            far *= 2
    return plan


def to_rows(block, rows):
    return block.astype(F32).reshape(rows, block.shape[-1])


def contract(a, b, dims):
    return lax.dot_general(a, b, (dims, ((), ())), preferred_element_type=F32)


def kernel(
    n_ha, n_wa, plan,
    table, q_ref, k_ref, v_ref, g_ref, norm_ref, delta_ref, tk_ref, tv_ref,
    dq_ref, dk_ref, dv_ref, dtk_ref, dtv_ref,
    stage, hcol, hrow, hcor, ret, rrow, rcol, own, dq_acc, mask, norm, delta, tx, tb, *rest,
):
    trecv = rest[: len(plan)]
    (col_s, col_r, row_s, row_r, cor_s, cor_r, rr_s, rr_r, rc_s, rc_r, t_s, t_r, u_s, u_r) = rest[len(plan):]
    frames, tile, _, width = q_ref.shape
    cells = frames * tile * tile
    text = tk_ref.shape[0]
    heads = width // HDIM
    part = width // GROUPS
    per = heads // GROUPS
    bands = tile // HALO
    scale = 1.0 / math.sqrt(HDIM)
    ha, wa = lax.axis_index("ha"), lax.axis_index("wa")
    ha_of = [{"ha": lax.rem(ha + n_ha - 1, n_ha)}, {"ha": lax.rem(ha + 1, n_ha)}]
    wa_of = [{"wa": lax.rem(wa + n_wa - 1, n_wa)}, {"wa": lax.rem(wa + 1, n_wa)}]
    partners, bits = [], []
    for axis, far, _, _, _ in plan:
        at = ha if axis == "ha" else wa
        bit = lax.rem(lax.div(at, far), 2)
        bits.append(bit)
        partners.append({axis: at + far * (1 - 2 * bit)})

    barrier = pltpu.get_barrier_semaphore()
    greeted = ha_of + wa_of + partners
    for other in greeted:
        pl.semaphore_signal(barrier, inc=1, device_id=other, device_id_type=MESH)

    def cols(g):
        return slice(g * part, (g + 1) * part)

    def remote(src, dst, s, r, device):
        return pltpu.make_async_remote_copy(
            src_ref=src, dst_ref=dst, send_sem=s, recv_sem=r, device_id=device, device_id_type=MESH
        )

    border = 2 * bands * frames * HALO * HALO

    def cell_of(j):
        side = lax.div(j, border // 2)
        band = lax.rem(lax.div(j, frames * HALO * HALO), bands)
        frame = lax.rem(lax.div(j, HALO * HALO), frames)
        row = band * HALO + lax.rem(lax.div(j, HALO), HALO)
        col = lax.rem(j, HALO) + side * (tile - HALO)
        return frame * tile * tile + row * tile + col

    lane = lax.broadcasted_iota(jnp.int32, (border, cells), 1)
    pick = (lane == cell_of(lax.broadcasted_iota(jnp.int32, (border, cells), 0))).astype(F32).astype(BF16)
    back_row = lax.broadcasted_iota(jnp.int32, (cells, 3 * border), 0)
    back_lane = lax.broadcasted_iota(jnp.int32, (cells, 3 * border), 1)
    put_back = (back_row == cell_of(lax.rem(back_lane, border))).astype(F32).astype(BF16)

    col_copy, row_copy, cor_copy, rr_copy, rc_copy = {}, {}, {}, {}, {}
    for g in range(GROUPS):
        for kv, ref in enumerate((k_ref, v_ref)):
            full = to_rows(ref[:, :, :, cols(g)], cells).astype(BF16)
            strip = contract(pick, full, ((1,), (0,)))
            stage[g, kv] = strip.reshape(2, bands, frames * HALO * HALO, part).astype(BF16)
        if g == 0:
            pl.semaphore_wait(barrier, len(greeted))
        for d in range(2):
            c = remote(stage.at[g, :, d], hcol.at[g, :, 1 - d], col_s.at[g, d], col_r.at[g, 1 - d], wa_of[d])
            c.start()
            col_copy[g, d] = c
        for v in range(2):
            for kv, ref in enumerate((k_ref, v_ref)):
                lo = v * (tile - HALO)
                c = remote(
                    ref.at[:, lo:lo + HALO, :, cols(g)], hrow.at[g, kv, 1 - v],
                    row_s.at[g, v, kv], row_r.at[g, 1 - v, kv], ha_of[v],
                )
                c.start()
                row_copy[g, v, kv] = c

    spread = (
        lax.rem(lax.broadcasted_iota(jnp.int32, (tile, cells), 1), tile)
        == lax.broadcasted_iota(jnp.int32, (tile, cells), 0)
    ).astype(F32)
    lines = frames * tile
    stat_shape = (heads * lines, cells)
    keep = lax.rem(lax.broadcasted_iota(jnp.int32, stat_shape, 0), lines) == lax.div(
        lax.broadcasted_iota(jnp.int32, stat_shape, 1), tile
    )
    for src, dst in ((norm_ref, norm), (delta_ref, delta)):
        wide = jnp.dot(src[...], spread, precision=lax.Precision.HIGHEST, preferred_element_type=F32)
        dst[...] = jnp.where(keep, wide, 0.0).reshape(heads, lines, cells).sum(axis=1)

    def live(block):
        return table[ha, wa, block].astype(F32)

    at = 0
    for block, rows in ((1, 32), (0, 8), (2, 8), (7, 32), (6, 8), (8, 8), (3, 32), (5, 32)):
        mask[at:at + rows, :] = jnp.full((rows, cells), live(block), F32)
        at += rows
    own_live = live(4)

    def attend(keys, values, h, masking):
        here = slice(h * HDIM, (h + 1) * HDIM)
        qh = to_rows(q_ref[:, :, :, here], cells).astype(BF16)
        gh = to_rows(g_ref[:, :, :, here], cells).astype(BF16)
        s = contract(keys, qh, ((1,), (1,))) * scale
        p = masking(jnp.exp(s - norm[h:h + 1, :]))
        dp = contract(values, gh, ((1,), (1,)))
        ds = (p * (dp - delta[h:h + 1, :])).astype(BF16)
        dv = contract(p.astype(BF16), gh, ((1,), (0,)))
        dk = contract(ds, qh, ((1,), (0,)))
        dq = contract(ds, keys, ((0,), (0,)))
        return dq, dk, dv

    def local(g):
        for h in range(g * per, (g + 1) * per):
            here = slice(h * HDIM, (h + 1) * HDIM)
            keys = jnp.concatenate([to_rows(k_ref[:, :, :, here], cells), tk_ref[:, here].astype(F32)], 0).astype(BF16)
            values = jnp.concatenate([to_rows(v_ref[:, :, :, here], cells), tv_ref[:, here].astype(F32)], 0).astype(BF16)
            dq, dk, dv = attend(
                keys, values, h, lambda p: jnp.concatenate([p[:cells] * own_live, p[cells:]], 0)
            )
            dq_acc[:, here] = dq
            own[0, :, here] = dk[:cells]
            own[1, :, here] = dv[:cells]
            tx[: text // 8, :, here] = (dk[cells:] * scale).reshape(text // 8, 8, HDIM)
            tx[text // 8:, :, here] = dv[cells:].reshape(text // 8, 8, HDIM)

    def forward(g):
        for d in range(2):
            col_copy[g, d].wait()
        for d in range(2):
            for v in range(2):
                c = remote(
                    hcol.at[g, :, d, v * (bands - 1)], hcor.at[g, :, 1 - v, d],
                    cor_s.at[g, d, v], cor_r.at[g, d, 1 - v], ha_of[v],
                )
                c.start()
                cor_copy[g, d, v] = c

    def halo(g):
        for v in range(2):
            for kv in range(2):
                row_copy[g, v, kv].wait()
            for d in range(2):
                cor_copy[g, d, v].wait()
        for h in range(per):
            here = slice(h * HDIM, (h + 1) * HDIM)
            absolute = slice((g * per + h) * HDIM, (g * per + h + 1) * HDIM)
            sides = []
            for kv in range(2):
                pieces = []
                for v in range(2):
                    pieces.append(to_rows(hrow[g, kv, v, :, :, :, here], frames * HALO * tile))
                    pieces.append(to_rows(hcor[g, kv, v, :, :, here], 2 * frames * HALO * HALO))
                pieces.append(to_rows(hcol[g, kv, :, :, :, here], border))
                sides.append(jnp.concatenate(pieces, 0).astype(BF16))
            dq, dk, dv = attend(sides[0], sides[1], g * per + h, lambda p: p * mask[...])
            dq_acc[:, absolute] += dq
            ret[g, 0, :, :, here] = dk.reshape(ret.shape[2], 8, HDIM)
            ret[g, 1, :, :, here] = dv.reshape(ret.shape[2], 8, HDIM)
        for v in range(2):
            c = remote(ret.at[g, :, 6 * v:6 * v + 6], rrow.at[g, 1 - v], rr_s.at[g, v], rr_r.at[g, 1 - v], ha_of[v])
            c.start()
            rr_copy[g, v] = c
        dq_ref[:, :, :, cols(g)] = (dq_acc[:, cols(g)] * scale).reshape(frames, tile, tile, part).astype(BF16)

    def fold_rows(g):
        for v in range(2):
            rr_copy[g, v].wait()
        for v in range(2):
            for kv in range(2):
                for d in range(2):
                    ret[g, kv, 12 + 4 * d + 3 * v] += rrow[g, v, kv, 4 + d]
        for d in range(2):
            c = remote(
                ret.at[g, :, 12 + 4 * d:16 + 4 * d], rcol.at[g, :, 1 - d],
                rc_s.at[g, d], rc_r.at[g, 1 - d], wa_of[d],
            )
            c.start()
            rc_copy[g, d] = c
        for v in range(2):
            for kv in range(2):
                for f in range(frames):
                    lo = f * tile * tile + v * (tile - HALO) * tile
                    own[kv, lo:lo + HALO * tile, cols(g)] += rrow[g, v, kv, 2 * f:2 * f + 2].reshape(HALO * tile, part)

    def fold_cols(g):
        for d in range(2):
            rc_copy[g, d].wait()
        for kv, out in enumerate((dk_ref, dv_ref)):
            came = rcol[g, kv].reshape(border, part)
            first = came.astype(BF16)
            left = came - first.astype(F32)
            second = left.astype(BF16)
            third = (left - second.astype(F32)).astype(BF16)
            total = own[kv, :, cols(g)] + contract(
                put_back, jnp.concatenate([first, second, third], 0), ((1,), (0,))
            )
            if kv == 0:
                total = total * scale
            out[:, :, :, cols(g)] = total.reshape(frames, tile, tile, part).astype(BF16)

    region = {"row": 0, "rows": 2 * text // 8, "col": 0, "cols": width}
    sums, regions = [], []

    def text_send(i):
        _, _, rows, wide, how = plan[i]
        regions.append(dict(region))
        row, col, bit = region["row"], region["col"], bits[i]
        send_row, send_col = row, col
        if how == "rows":
            send_row = row + (1 - bit) * rows
            region.update(row=row + bit * rows, rows=rows)
        elif how == "cols":
            send_col = col + (1 - bit) * wide
            region.update(col=col + bit * wide, cols=wide)
        c = remote(area(tx, send_row, rows, send_col, wide), trecv[i], t_s.at[i], t_r.at[i], partners[i])
        c.start()
        sums.append(c)

    def area(ref, row, rows, col, wide):
        lanes = pl.ds(pl.multiple_of(col, 128), wide) if not isinstance(col, int) else pl.ds(col, wide)
        return ref.at[pl.ds(row, rows), :, lanes]

    def mine(ref):
        return area(ref, region["row"], region["rows"], region["col"], region["cols"])

    def text_add(i):
        sums[i].wait()
        kept = mine(tx)
        kept[...] += trecv[i][...]

    gathers = []

    def text_spread(i):
        if i == len(plan) - 1:
            mine(tb)[...] = mine(tx)[...].astype(BF16)
        if plan[i][4] == "none":
            gathers.append(None)
            return
        c = remote(mine(tb), mine(tb), u_s.at[i], u_r.at[i], partners[i])
        c.start()
        gathers.append(c)

    def text_join(i):
        c = gathers.pop()
        if c is not None:
            c.wait()
        region.update(regions[i])

    steps = []
    for i in range(len(plan)):
        steps += [functools.partial(text_send, i), functools.partial(text_add, i)]
    for i in reversed(range(len(plan))):
        steps += [functools.partial(text_spread, i), functools.partial(text_join, i)]
    waiting = []
    for n in range(0, len(steps)):
        if n % 2 == 0:
            waiting.append([steps[n]])
            if n > 0:
                waiting[-1].insert(0, steps[n - 1])
    waiting.append([steps[-1]])

    def text_step():
        if waiting:
            for step in waiting.pop(0):
                step()

    local(0)
    local(1)
    forward(0)
    for g in range(2, GROUPS):
        local(g)
    text_step()
    forward(1)
    halo(0)
    text_step()
    for g in range(1, GROUPS):
        if g + 1 < GROUPS:
            forward(g + 1)
        halo(g)
        text_step()
        fold_rows(g - 1)
        text_step()
    fold_rows(GROUPS - 1)
    for g in range(GROUPS):
        text_step()
        fold_cols(g)
    while waiting:
        text_step()
    dtk_ref[...] = to_rows(tb[: text // 8], text).astype(BF16)
    dtv_ref[...] = to_rows(tb[text // 8:], text).astype(BF16)


def solution(mesh):
    n_ha, n_wa = mesh.shape["ha"], mesh.shape["wa"]

    def local(queries, keys, values, out_grad, log_norm, delta_rows, text_keys, text_values, window_table):
        frames, tile, _, width = queries.shape
        heads = width // HDIM
        text = text_keys.shape[0]
        cells = frames * tile * tile
        part = width // GROUPS
        bands = tile // HALO
        block = frames * HALO * HALO
        halo_blocks = (4 * HALO * tile * frames + 4 * block) // 8
        plan = text_plan(n_ha, n_wa, 2 * text // 8, width)
        received = []
        for _, _, rows, wide, _ in plan:
            received.append(pltpu.VMEM((rows, 8, wide), F32))
        sem = pltpu.SemaphoreType.DMA
        vmem = pl.BlockSpec(memory_space=pltpu.VMEM)
        outs = (
            jax.ShapeDtypeStruct(queries.shape, BF16),
            jax.ShapeDtypeStruct(queries.shape, BF16),
            jax.ShapeDtypeStruct(queries.shape, BF16),
            jax.ShapeDtypeStruct(text_keys.shape, BF16),
            jax.ShapeDtypeStruct(text_keys.shape, BF16),
        )
        return pl.pallas_call(
            functools.partial(kernel, n_ha, n_wa, plan),
            out_shape=outs,
            in_specs=[pl.BlockSpec(memory_space=pltpu.SMEM)] + [vmem] * 8,
            out_specs=[vmem] * 5,
            scratch_shapes=[
                pltpu.VMEM((GROUPS, 2, 2, bands, block, part), BF16),
                pltpu.VMEM((GROUPS, 2, 2, bands, block, part), BF16),
                pltpu.VMEM((GROUPS, 2, 2, frames, HALO, tile, part), BF16),
                pltpu.VMEM((GROUPS, 2, 2, 2, block, part), BF16),
                pltpu.VMEM((GROUPS, 2, halo_blocks, 8, part), F32),
                pltpu.VMEM((GROUPS, 2, 2, 6, 8, part), F32),
                pltpu.VMEM((GROUPS, 2, 2, bands, block, part), F32),
                pltpu.VMEM((2, cells, width), F32),
                pltpu.VMEM((cells, width), F32),
                pltpu.VMEM((8 * halo_blocks, cells), F32),
                pltpu.VMEM((heads, cells), F32),
                pltpu.VMEM((heads, cells), F32),
                pltpu.VMEM((2 * text // 8, 8, width), F32),
                pltpu.VMEM((2 * text // 8, 8, width), BF16),
                *received,
                sem((GROUPS, 2)), sem((GROUPS, 2)),
                sem((GROUPS, 2, 2)), sem((GROUPS, 2, 2)),
                sem((GROUPS, 2, 2)), sem((GROUPS, 2, 2)),
                sem((GROUPS, 2)), sem((GROUPS, 2)),
                sem((GROUPS, 2)), sem((GROUPS, 2)),
                sem((len(plan),)), sem((len(plan),)),
                sem((len(plan),)), sem((len(plan),)),
            ],
            compiler_params=pltpu.CompilerParams(
                collective_id=0, has_side_effects=True, vmem_limit_bytes=56 * 1024 * 1024
            ),
        )(
            window_table, queries, keys, values, out_grad,
            log_norm.reshape(-1, tile), delta_rows.reshape(-1, tile), text_keys, text_values,
        )

    tile_spec = P("group", "ha", "wa", None)
    stat_spec = P(None, "group", "ha", "wa")
    text_spec = P("group", None)
    return jax.shard_map(
        local,
        mesh=mesh,
        in_specs=(tile_spec,) * 4 + (stat_spec,) * 2 + (text_spec,) * 2 + (P(),),
        out_specs=(tile_spec,) * 3 + (text_spec,) * 2,
        check_vma=False,
    )
```

time: 152 us -> 58.5 us (0.38)
  blocking collectives: 73.5 us -> 0 us
  Pallas kernels: 0 us -> 49.5 us
  waiting for transfers between devices: 23.1 us -> 0 us
  local copies, waits for them, and re-layouts: 30 us -> 7.99 us
  starting transfers between devices: 11.3 us -> 0 us
  other arithmetic: 6.52 us -> 0 us
  matrix products: 6.17 us -> 0 us
    psum x1 -> x0, blocking collectives: 73.5 us -> none  [local(): text_total = lax.psum(jnp.stack((text_key, text_value)), ('ha', 'wa'))]
    pallas_call x0 -> x1, Pallas kernels: none -> 49.5 us  [local(): pl.pallas_call(functools.partial(kernel, n_ha, n_wa, plan), out_shape=out...]
    ppermute x8 -> x0, waiting for transfers between devices: 23.1 us -> none  [the longest x4 23.1 us: passed_along(): return lax.ppermute(value, axis, pairs)]
    ppermute x8 -> x0, starting transfers between devices: 11.3 us -> none  [the longest x4 4.38 us: passed_along(): return lax.ppermute(value, axis, pairs)]
    another operation x5 -> x0, local copies, waits for them, and re-layouts: 8.28 us -> none  [the longest x3 5.81 us: local(): jnp.stack((video_key, video_value))]
    dot_general x12 -> x0, matrix products: 6.17 us -> none  [the longest x2 1.83 us: tile_grads(): jnp.einsum('hqk,qhd->khd', probs_half, cotangent_rows, preferred_element_...]
    unnamed x29 -> x17, local copies, waits for them, and re-layouts: 2.91 us -> 7.99 us
    transpose x1 -> x0, local copies, waits for them, and re-layouts: 3.98 us -> none  [tile_grads(): jnp.einsum('hqk,qhd->khd', probs_half, cotangent_rows, preferred_element_...]
  transfers between devices with their start and end apart: 8 -> 0, of which waited for: 4 -> 0; matrix products, arithmetic and copies ran while one was open for 8% -> 0% of each run, Pallas kernels for 0% -> 0%
where the time goes in v1:
time: 58.5 us; the launch traced here: 58.2 us
  Pallas kernels  49.5 us (85%)
  local copies, waits for them, and re-layouts  7.99 us (14%)
  between operations  0.66 us (1%)
    pallas_call x1, Pallas kernels, local(): pl.pallas_call(functools.partial(kernel, n_ha, n_wa, plan), out_shape=out...  49.5 us
    unnamed x17, local copies, waits for them, and re-layouts  7.99 us

profile of v1, /device:TPU:0, one launch (start us, length us, event | category | flops | bytes accessed | tf_op | source)
XLA Modules:
  0.0 58.2 jit_solution(14211212253575246601)
XLA Ops:
  0.6 0.0 copy-start.4
  0.6 1.7 %copy.14 = f32[12,2,8,8]{3,2,1,0:T(8,128)} copy(f32[12,2,8,8]{0,3,2,1:T(8,128)} %param.13) | data formatting | bytes 12288 | tf_op args[4]
  2.3 0.0 copy-done.4
  2.3 0.8 %copy.15 = f32[12,2,8,8]{3,2,1,0:T(8,128)} copy(f32[12,2,8,8]{0,3,2,1:T(8,128)S(1)} %copy-done.4) | data formatting | bytes 12288 | tf_op args[5]
  3.1 49.5 %shard_map.128 = (bf16[2,8,8,1536]{3,2,1,0:T(8,128)(2,1)}, bf16[2,8,8,1536]{3,2,1,0:T(8,128)(2,1)}, bf16[2,8,8,1536]{3,2,1,0:T(8,128)(2,1)}, bf16[32,1536]{1,0:T(8,128)(2,1)}, bf16[32,1536]{1,0:T(8,128)(2,1)}) custom-call(s32[4,4,9]{2,1,0:T(4,128)} %table.1, bf16[2,8,8,1536]{3,2,1,0:T(8,128)(2,1)} %q_ref.1, bf16[2,8,8,1536]{3,2,1,0:T(8,128)(2,1)} %k_ref.1, ...), custom_call_target="tpu_custom_call" | custom-call | tf_op jit(solution)/shard_map/pallas_call | solution.py:362
  52.7 0.0 copy-start.1
  52.7 1.8 %copy.21 = bf16[2,8,8,1536]{3,2,1,0:T(8,128)(2,1)} copy(bf16[2,8,8,1536]{3,2,1,0:T(8,128)(2,1)} %get-tuple-element.10) | data formatting | bytes 786432
  54.5 0.0 copy-done.1
  54.5 0.0 copy-start
  54.5 0.7 %copy.22 = bf16[2,8,8,1536]{3,2,1,0:T(8,128)(2,1)} copy(bf16[2,8,8,1536]{3,2,1,0:T(8,128)(2,1)S(1)} %copy-done.1) | data formatting | bytes 786432
  55.3 0.4 copy-done
  55.6 0.0 copy-start.3
  55.6 0.7 %copy.23 = bf16[2,8,8,1536]{3,2,1,0:T(8,128)(2,1)} copy(bf16[2,8,8,1536]{3,2,1,0:T(8,128)(2,1)S(1)} %copy-done) | data formatting | bytes 786432
  56.4 0.2 copy-done.3
  56.6 0.0 copy-start.2
  56.6 0.6 %copy.24 = bf16[32,1536]{1,0:T(8,128)(2,1)} copy(bf16[32,1536]{1,0:T(8,128)(2,1)S(1)} %copy-done.3) | data formatting | bytes 196608
  57.3 0.3 copy-done.2
  57.5 0.6 %copy.25 = bf16[32,1536]{1,0:T(8,128)(2,1)} copy(bf16[32,1536]{1,0:T(8,128)(2,1)S(1)} %copy-done.2) | data formatting | bytes 196608
Async XLA Ops:
  0.6 1.7 %copy-start.4 = (f32[12,2,8,8]{0,3,2,1:T(8,128)S(1)}, f32[12,2,8,8]{0,3,2,1:T(8,128)}, u32[]{:S(2)}) copy-start(f32[12,2,8,8]{0,3,2,1:T(8,128)} %param.14) | copy-start | bytes 18436
  52.7 1.8 %copy-start.1 = (bf16[2,8,8,1536]{3,2,1,0:T(8,128)(2,1)S(1)}, bf16[2,8,8,1536]{3,2,1,0:T(8,128)(2,1)}, u32[]{:S(2)}) copy-start(bf16[2,8,8,1536]{3,2,1,0:T(8,128)(2,1)} %get-tuple-element.11) | copy-start | bytes 1179652
  54.5 1.1 %copy-start = (bf16[2,8,8,1536]{3,2,1,0:T(8,128)(2,1)S(1)}, bf16[2,8,8,1536]{3,2,1,0:T(8,128)(2,1)}, u32[]{:S(2)}) copy-start(bf16[2,8,8,1536]{3,2,1,0:T(8,128)(2,1)} %get-tuple-element.12) | copy-start | bytes 1179652
  55.6 1.0 %copy-start.3 = (bf16[32,1536]{1,0:T(8,128)(2,1)S(1)}, bf16[32,1536]{1,0:T(8,128)(2,1)}, u32[]{:S(2)}) copy-start(bf16[32,1536]{1,0:T(8,128)(2,1)} %get-tuple-element.13) | copy-start | bytes 294916
  56.6 0.9 %copy-start.2 = (bf16[32,1536]{1,0:T(8,128)(2,1)S(1)}, bf16[32,1536]{1,0:T(8,128)(2,1)}, u32[]{:S(2)}) copy-start(bf16[32,1536]{1,0:T(8,128)(2,1)} %get-tuple-element.14) | copy-start | bytes 294916

commit v2 on v1

--- a/solution.py
+++ b/solution.py
@@ -45,10 +45,10 @@
     n_ha, n_wa, plan,
     table, q_ref, k_ref, v_ref, g_ref, norm_ref, delta_ref, tk_ref, tv_ref,
     dq_ref, dk_ref, dv_ref, dtk_ref, dtv_ref,
-    stage, hcol, hrow, hcor, ret, rrow, rcol, own, dq_acc, mask, norm, delta, tx, tb, *rest,
+    stage, hcol, hrow, hcor, ret, rrow, rcor, rcol, own, dq_acc, mask, norm, delta, tx, tb, *rest,
 ):
     trecv = rest[: len(plan)]
-    (col_s, col_r, row_s, row_r, cor_s, cor_r, rr_s, rr_r, rc_s, rc_r, t_s, t_r, u_s, u_r) = rest[len(plan):]
+    (col_s, col_r, row_s, row_r, cor_s, cor_r, rr_s, rr_r, rc_s, rc_r, mid_s, mid_r, rq_s, rq_r, t_s, t_r, u_s, u_r) = rest[len(plan):]
     frames, tile, _, width = q_ref.shape
     cells = frames * tile * tile
     text = tk_ref.shape[0]
@@ -56,6 +56,7 @@
     part = width // GROUPS
     per = heads // GROUPS
     bands = tile // HALO
+    rim = ret.shape[2] - 2 * bands
     scale = 1.0 / math.sqrt(HDIM)
     ha, wa = lax.axis_index("ha"), lax.axis_index("wa")
     ha_of = [{"ha": lax.rem(ha + n_ha - 1, n_ha)}, {"ha": lax.rem(ha + 1, n_ha)}]
@@ -96,7 +97,7 @@
     back_lane = lax.broadcasted_iota(jnp.int32, (cells, 3 * border), 1)
     put_back = (back_row == cell_of(lax.rem(back_lane, border))).astype(F32).astype(BF16)
 
-    col_copy, row_copy, cor_copy, rr_copy, rc_copy = {}, {}, {}, {}, {}
+    col_copy, row_copy, cor_copy, rr_copy, rc_copy, mid_copy, rq_copy = {}, {}, {}, {}, {}, {}, {}
     for g in range(GROUPS):
         for kv, ref in enumerate((k_ref, v_ref)):
             full = to_rows(ref[:, :, :, cols(g)], cells).astype(BF16)
@@ -118,24 +119,18 @@
                 c.start()
                 row_copy[g, v, kv] = c
 
-    spread = (
-        lax.rem(lax.broadcasted_iota(jnp.int32, (tile, cells), 1), tile)
-        == lax.broadcasted_iota(jnp.int32, (tile, cells), 0)
-    ).astype(F32)
-    lines = frames * tile
-    stat_shape = (heads * lines, cells)
-    keep = lax.rem(lax.broadcasted_iota(jnp.int32, stat_shape, 0), lines) == lax.div(
-        lax.broadcasted_iota(jnp.int32, stat_shape, 1), tile
-    )
+    square = (cells, cells)
+    same = (lax.broadcasted_iota(jnp.int32, square, 0) == lax.broadcasted_iota(jnp.int32, square, 1)).astype(F32)
     for src, dst in ((norm_ref, norm), (delta_ref, delta)):
-        wide = jnp.dot(src[...], spread, precision=lax.Precision.HIGHEST, preferred_element_type=F32)
-        dst[...] = jnp.where(keep, wide, 0.0).reshape(heads, lines, cells).sum(axis=1)
+        dst[...] = lax.dot_general(
+            src[...], same, (((0,), (0,)), ((), ())), precision=lax.Precision.HIGHEST, preferred_element_type=F32
+        )
 
     def live(block):
         return table[ha, wa, block].astype(F32)
 
     at = 0
-    for block, rows in ((1, 32), (0, 8), (2, 8), (7, 32), (6, 8), (8, 8), (3, 32), (5, 32)):
+    for block, rows in ((1, 32), (7, 32), (0, 8), (2, 8), (6, 8), (8, 8), (3, 32), (5, 32)):
         mask[at:at + rows, :] = jnp.full((rows, cells), live(block), F32)
         at += rows
     own_live = live(4)
@@ -153,19 +148,22 @@
         dq = contract(ds, keys, ((0,), (0,)))
         return dq, dk, dv
 
+    def texts():
+        for h in range(heads):
+            here = slice(h * HDIM, (h + 1) * HDIM)
+            dq, dk, dv = attend(tk_ref[:, here], tv_ref[:, here], h, lambda p: p)
+            dq_acc[:, here] = dq
+            tx[: text // 8, :, here] = (dk * scale).reshape(text // 8, 8, HDIM)
+            tx[text // 8:, :, here] = dv.reshape(text // 8, 8, HDIM)
+
     def local(g):
         for h in range(g * per, (g + 1) * per):
             here = slice(h * HDIM, (h + 1) * HDIM)
-            keys = jnp.concatenate([to_rows(k_ref[:, :, :, here], cells), tk_ref[:, here].astype(F32)], 0).astype(BF16)
-            values = jnp.concatenate([to_rows(v_ref[:, :, :, here], cells), tv_ref[:, here].astype(F32)], 0).astype(BF16)
-            dq, dk, dv = attend(
-                keys, values, h, lambda p: jnp.concatenate([p[:cells] * own_live, p[cells:]], 0)
-            )
-            dq_acc[:, here] = dq
-            own[0, :, here] = dk[:cells]
-            own[1, :, here] = dv[:cells]
-            tx[: text // 8, :, here] = (dk[cells:] * scale).reshape(text // 8, 8, HDIM)
-            tx[text // 8:, :, here] = dv[cells:].reshape(text // 8, 8, HDIM)
+            keys, values = (to_rows(ref[:, :, :, here], cells).astype(BF16) for ref in (k_ref, v_ref))
+            dq, dk, dv = attend(keys, values, h, lambda p: p * own_live)
+            dq_acc[:, here] += dq
+            own[0, :, here] = dk
+            own[1, :, here] = dv
 
     def forward(g):
         for d in range(2):
@@ -179,56 +177,93 @@
                 c.start()
                 cor_copy[g, d, v] = c
 
-    def halo(g):
-        for v in range(2):
-            for kv in range(2):
-                row_copy[g, v, kv].wait()
-            for d in range(2):
-                cor_copy[g, d, v].wait()
+    def columns(g):
         for h in range(per):
             here = slice(h * HDIM, (h + 1) * HDIM)
             absolute = slice((g * per + h) * HDIM, (g * per + h + 1) * HDIM)
-            sides = []
+            keys, values = (to_rows(hcol[g, kv, :, :, :, here], border).astype(BF16) for kv in range(2))
+            dq, dk, dv = attend(keys, values, g * per + h, lambda p: p * mask[8 * rim:])
+            dq_acc[:, absolute] += dq
+            ret[g, 0, rim:, :, here] = dk.reshape(2 * bands, 8, HDIM)
+            ret[g, 1, rim:, :, here] = dv.reshape(2 * bands, 8, HDIM)
+        for d in range(2):
+            lo = rim + d * bands
+            c = remote(
+                ret.at[g, :, lo + 1:lo + bands - 1], rcol.at[g, :, 1 - d, 1:bands - 1],
+                mid_s.at[g, d], mid_r.at[g, 1 - d], wa_of[d],
+            )
+            c.start()
+            mid_copy[g, d] = c
+
+    def pieces_pass(g, refs_of, lo, size, weights):
+        for h in range(per):
+            here = slice(h * HDIM, (h + 1) * HDIM)
+            absolute = slice((g * per + h) * HDIM, (g * per + h + 1) * HDIM)
+            keys, values = (refs_of(kv, here).astype(BF16) for kv in range(2))
+            dq, dk, dv = attend(keys, values, g * per + h, lambda p: p * weights)
+            dq_acc[:, absolute] += dq
+            ret[g, 0, lo:lo + size, :, here] = dk.reshape(size, 8, HDIM)
+            ret[g, 1, lo:lo + size, :, here] = dv.reshape(size, 8, HDIM)
+
+    def strips(g):
+        for v in range(2):
             for kv in range(2):
-                pieces = []
-                for v in range(2):
-                    pieces.append(to_rows(hrow[g, kv, v, :, :, :, here], frames * HALO * tile))
-                    pieces.append(to_rows(hcor[g, kv, v, :, :, here], 2 * frames * HALO * HALO))
-                pieces.append(to_rows(hcol[g, kv, :, :, :, here], border))
-                sides.append(jnp.concatenate(pieces, 0).astype(BF16))
-            dq, dk, dv = attend(sides[0], sides[1], g * per + h, lambda p: p * mask[...])
-            dq_acc[:, absolute] += dq
-            ret[g, 0, :, :, here] = dk.reshape(ret.shape[2], 8, HDIM)
-            ret[g, 1, :, :, here] = dv.reshape(ret.shape[2], 8, HDIM)
-        for v in range(2):
-            c = remote(ret.at[g, :, 6 * v:6 * v + 6], rrow.at[g, 1 - v], rr_s.at[g, v], rr_r.at[g, 1 - v], ha_of[v])
+                row_copy[g, v, kv].wait()
+        wide = 2 * frames * HALO * tile
+        pieces_pass(g, lambda kv, here: to_rows(hrow[g, kv, :, :, :, :, here], wide), 0, wide // 8, mask[:wide])
+        half = wide // 16
+        for v in range(2):
+            c = remote(
+                ret.at[g, :, half * v:half * (v + 1)], rrow.at[g, 1 - v], rr_s.at[g, v], rr_r.at[g, 1 - v], ha_of[v]
+            )
             c.start()
             rr_copy[g, v] = c
-        dq_ref[:, :, :, cols(g)] = (dq_acc[:, cols(g)] * scale).reshape(frames, tile, tile, part).astype(BF16)
-
-    def fold_rows(g):
-        for v in range(2):
-            rr_copy[g, v].wait()
-        for v in range(2):
-            for kv in range(2):
-                for d in range(2):
-                    ret[g, kv, 12 + 4 * d + 3 * v] += rrow[g, v, kv, 4 + d]
-        for d in range(2):
+
+    def corners(g):
+        for v in range(2):
+            for d in range(2):
+                cor_copy[g, d, v].wait()
+        pieces_pass(
+            g, lambda kv, here: to_rows(hcor[g, kv, :, :, :, here], 32), rim - 4, 4, mask[8 * (rim - 4):8 * rim]
+        )
+        for v in range(2):
             c = remote(
-                ret.at[g, :, 12 + 4 * d:16 + 4 * d], rcol.at[g, :, 1 - d],
-                rc_s.at[g, d], rc_r.at[g, 1 - d], wa_of[d],
+                ret.at[g, :, rim - 4 + 2 * v:rim - 2 + 2 * v], rcor.at[g, 1 - v],
+                rq_s.at[g, v], rq_r.at[g, 1 - v], ha_of[v],
             )
             c.start()
-            rc_copy[g, d] = c
+            rq_copy[g, v] = c
+
+    def fold_corners(g):
+        for v in range(2):
+            rq_copy[g, v].wait()
+        for v in range(2):
+            for d in range(2):
+                at = rim + bands * d + (bands - 1) * v
+                for kv in range(2):
+                    ret[g, kv, at] += rcor[g, v, kv, d]
+                c = remote(
+                    ret.at[g, :, at], rcol.at[g, :, 1 - d, v * (bands - 1)],
+                    rc_s.at[g, d, v], rc_r.at[g, 1 - d, v], wa_of[d],
+                )
+                c.start()
+                rc_copy[g, d, v] = c
+
+    def fold_rows(g):
+        for v in range(2):
+            rr_copy[g, v].wait()
         for v in range(2):
             for kv in range(2):
                 for f in range(frames):
                     lo = f * tile * tile + v * (tile - HALO) * tile
                     own[kv, lo:lo + HALO * tile, cols(g)] += rrow[g, v, kv, 2 * f:2 * f + 2].reshape(HALO * tile, part)
+        dq_ref[:, :, :, cols(g)] = (dq_acc[:, cols(g)] * scale).reshape(frames, tile, tile, part).astype(BF16)
 
     def fold_cols(g):
         for d in range(2):
-            rc_copy[g, d].wait()
+            mid_copy[g, d].wait()
+            for v in range(2):
+                rc_copy[g, d, v].wait()
         for kv, out in enumerate((dk_ref, dv_ref)):
             came = rcol[g, kv].reshape(border, part)
             first = came.astype(BF16)
@@ -308,30 +343,57 @@
             for step in waiting.pop(0):
                 step()
 
+    texts()
+    text_step()
     local(0)
     local(1)
+    text_step()
+    local(2)
+    local(3)
+    strips(0)
+    strips(1)
+    text_step()
     forward(0)
-    for g in range(2, GROUPS):
-        local(g)
-    text_step()
+    columns(0)
     forward(1)
-    halo(0)
-    text_step()
-    for g in range(1, GROUPS):
-        if g + 1 < GROUPS:
-            forward(g + 1)
-        halo(g)
-        text_step()
-        fold_rows(g - 1)
-        text_step()
-    fold_rows(GROUPS - 1)
-    for g in range(GROUPS):
-        text_step()
-        fold_cols(g)
+    columns(1)
+    corners(0)
+    text_step()
+    forward(2)
+    columns(2)
+    corners(1)
+    forward(3)
+    columns(3)
+    corners(2)
+    text_step()
+    fold_corners(0)
+    corners(3)
+    strips(2)
+    fold_corners(1)
+    strips(3)
+    fold_corners(2)
+    text_step()
+    fold_corners(3)
+    text_step()
+    fold_rows(0)
+    fold_rows(1)
+    fold_rows(2)
+    fold_rows(3)
+    fold_cols(0)
+    text_step()
+    fold_cols(1)
+    fold_cols(2)
+    fold_cols(3)
     while waiting:
         text_step()
     dtk_ref[...] = to_rows(tb[: text // 8], text).astype(BF16)
     dtv_ref[...] = to_rows(tb[text // 8:], text).astype(BF16)
+
+
+def hand_on(*refs):
+    count = len(refs) // 2
+    for source, target in zip(refs[:count], refs[count:]):
+        target[...] = source[...]
 
 
 def solution(mesh):
@@ -359,7 +421,7 @@
             jax.ShapeDtypeStruct(text_keys.shape, BF16),
             jax.ShapeDtypeStruct(text_keys.shape, BF16),
         )
-        return pl.pallas_call(
+        results = pl.pallas_call(
             functools.partial(kernel, n_ha, n_wa, plan),
             out_shape=outs,
             in_specs=[pl.BlockSpec(memory_space=pltpu.SMEM)] + [vmem] * 8,
@@ -370,7 +432,8 @@
                 pltpu.VMEM((GROUPS, 2, 2, frames, HALO, tile, part), BF16),
                 pltpu.VMEM((GROUPS, 2, 2, 2, block, part), BF16),
                 pltpu.VMEM((GROUPS, 2, halo_blocks, 8, part), F32),
-                pltpu.VMEM((GROUPS, 2, 2, 6, 8, part), F32),
+                pltpu.VMEM((GROUPS, 2, 2, 4, 8, part), F32),
+                pltpu.VMEM((GROUPS, 2, 2, 2, 8, part), F32),
                 pltpu.VMEM((GROUPS, 2, 2, bands, block, part), F32),
                 pltpu.VMEM((2, cells, width), F32),
                 pltpu.VMEM((cells, width), F32),
@@ -384,6 +447,8 @@
                 sem((GROUPS, 2, 2)), sem((GROUPS, 2, 2)),
                 sem((GROUPS, 2, 2)), sem((GROUPS, 2, 2)),
                 sem((GROUPS, 2)), sem((GROUPS, 2)),
+                sem((GROUPS, 2, 2)), sem((GROUPS, 2, 2)),
+                sem((GROUPS, 2)), sem((GROUPS, 2)),
                 sem((GROUPS, 2)), sem((GROUPS, 2)),
                 sem((len(plan),)), sem((len(plan),)),
                 sem((len(plan),)), sem((len(plan),)),
@@ -393,8 +458,16 @@
             ),
         )(
             window_table, queries, keys, values, out_grad,
-            log_norm.reshape(-1, tile), delta_rows.reshape(-1, tile), text_keys, text_values,
+            log_norm.transpose(1, 2, 3, 0).reshape(cells, heads), delta_rows.transpose(1, 2, 3, 0).reshape(cells, heads),
+            text_keys, text_values,
         )
+
+        return pl.pallas_call(
+            hand_on,
+            out_shape=outs,
+            in_specs=[vmem] * 5,
+            out_specs=[vmem] * 5,
+        )(*results)
 
     tile_spec = P("group", "ha", "wa", None)
     stat_spec = P(None, "group", "ha", "wa")

time: 58.5 us -> 45.2 us (0.77)
  local copies, waits for them, and re-layouts: 7.99 us -> 0 us
  Pallas kernels: 49.5 us -> 44.4 us
    unnamed x17 -> x0, local copies, waits for them, and re-layouts: 7.99 us -> none
    pallas_call x1, Pallas kernels: 49.5 us -> 42 us  [local(): pl.pallas_call(functools.partial(kernel, n_ha, n_wa, plan), out_shape=out...]
    pallas_call x0 -> x1, Pallas kernels: none -> 2.39 us  [local(): pl.pallas_call(hand_on, out_shape=outs, in_specs=[vmem] * 5, out_specs=[v...]
where the time goes in v2:
time: 45.2 us; the launch traced here: 45 us
  Pallas kernels  44.4 us (98%)
  between operations  0.64 us (1%)
    pallas_call x1, Pallas kernels, local(): pl.pallas_call(functools.partial(kernel, n_ha, n_wa, plan), out_shape=out...  42 us
    pallas_call x1, Pallas kernels, local(): pl.pallas_call(hand_on, out_shape=outs, in_specs=[vmem] * 5, out_specs=[v...  2.39 us

profile of v2, /device:TPU:0, one launch (start us, length us, event | category | flops | bytes accessed | tf_op | source)
XLA Modules:
  0.0 45.0 jit_solution(11831017784844602277)
XLA Ops:
  0.6 42.0 %shard_map.128 = (bf16[2,8,8,1536]{3,2,1,0:T(8,128)(2,1)}, bf16[2,8,8,1536]{3,2,1,0:T(8,128)(2,1)}, bf16[2,8,8,1536]{3,2,1,0:T(8,128)(2,1)}, bf16[32,1536]{1,0:T(8,128)(2,1)}, bf16[32,1536]{1,0:T(8,128)(2,1)}) custom-call(s32[4,4,9]{2,1,0:T(4,128)} %table.1, bf16[2,8,8,1536]{3,2,1,0:T(8,128)(2,1)} %q_ref.1, bf16[2,8,8,1536]{3,2,1,0:T(8,128)(2,1)} %k_ref.1, ...), custom_call_target="tpu_custom_call" | custom-call | tf_op jit(solution)/shard_map/pallas_call | solution.py:424
  42.6 2.4 %shard_map.129 = (bf16[2,8,8,1536]{3,2,1,0:T(8,128)(2,1)}, bf16[2,8,8,1536]{3,2,1,0:T(8,128)(2,1)}, bf16[2,8,8,1536]{3,2,1,0:T(8,128)(2,1)}, bf16[32,1536]{1,0:T(8,128)(2,1)}, bf16[32,1536]{1,0:T(8,128)(2,1)}) custom-call(bf16[2,8,8,1536]{3,2,1,0:T(8,128)(2,1)} %get-tuple-element.10.refs_0_, bf16[2,8,8,1536]{3,2,1,0:T(8,128)(2,1)} %get-tuple-element.11.refs_1_, ...), custom_call_target="tpu_custom_call" | custom-call | tf_op jit(solution)/shard_map/pallas_call | solution.py:465
